TPU v7x, 32 devices: a whole 2x2x4 slice. The times are simulated.
32 devices in a mesh: dp: 8 (over y, x, core), tp: 4 (over z).
Axes of the slice: x: 2, y: 2, z: 4, core: 2. Of those that a mesh axis runs over, the one named last changes fastest.
Arguments:
- inputs: bfloat16 [8, 768, 1280], P('dp', 'tp'), may hold values from -6 to 6
- saved_hidden: bfloat16 [8, 768, 5120], P('dp', None, 'tp'), may hold values from -8 to 8
- upstream: bfloat16 [8, 768, 1280], P('dp', 'tp'), may hold values from -6 to 6
- w_in: bfloat16 [1280, 5120], P(None, 'tp'), may hold values from -0.15625 to 0.15625
- w_out: bfloat16 [5120, 1280], P('tp'), may hold values from -0.078125 to 0.078125
- kernel: float32 [7, 1280], replicated, may hold values from -2 to 2
Outputs:
- grad_inputs: bfloat16 [8, 768, 1280], P('dp', 'tp')
- grad_w_in: float32 [1280, 5120], P(None, 'tp')
- grad_w_out: float32 [5120, 1280], P('tp')
- grad_bias: float32 [5120], P('tp')
- grad_kernel: float32 [7, 1280], replicated
All inputs are finite; a program needn't handle non-finite values.
Results may differ from a plain program's by a relative error of at most 0.02.
Values may be sent and summed in bfloat16 or wider, within the bound.
A program may use at most 128 MiB of HBM per device.

v0:
```python
import jax
import jax.numpy as jnp
from jax import lax
from jax.sharding import PartitionSpec as P

KW = 7


def with_halo(cells, sides, width):
    for axis, dim in sides:
        count = lax.axis_size(axis)
        ends = count - 1
        head = lax.slice_in_dim(cells, 0, width, axis=dim)
        tail = lax.slice_in_dim(cells, cells.shape[dim] - width, cells.shape[dim], axis=dim)
        cells = jnp.concatenate(
            [
                lax.ppermute(tail, axis, [(i, (i + 1) % count) for i in range(ends)]),
                cells,
                lax.ppermute(head, axis, [((i + 1) % count, i) for i in range(ends)]),
            ],
            axis=dim,
        )
    return cells


def gelu_exact(value):
    return jax.nn.gelu(value, approximate=False)


def convolve(padded, kernel, length):
    mixed = padded[3 : 3 + length].astype(jnp.float32)
    for tap in range(KW):
        mixed = mixed + kernel[tap] * padded[tap : tap + length].astype(jnp.float32)
    return mixed.astype(jnp.bfloat16)


def shards(inputs, saved_hidden, upstream, w_in, w_out, kernel):
    tokens = inputs[0]
    hidden = saved_hidden[0]
    grad_out = upstream[0]
    length = tokens.shape[0]
    piece = lax.all_gather(grad_out, "tp", axis=0, tiled=True)
    hidden_rows = hidden.astype(jnp.float32)
    back_rows = lax.dot_general(
        piece, w_out, (((1,), (1,)), ((), ())), preferred_element_type=jnp.float32
    )
    grad_rows = jax.vjp(gelu_exact, hidden_rows)[1](back_rows)[0].astype(jnp.bfloat16)
    buffer = grad_rows
    activated = gelu_exact(hidden_rows).astype(jnp.bfloat16)
    total = lax.dot_general(
        activated, piece, (((0,), (0,)), ((), ())), preferred_element_type=jnp.float32
    )
    grad_w_out = total
    grad_bias = jnp.sum(buffer.astype(jnp.float32), axis=0)
    summed = lax.psum_scatter(
        lax.dot_general(
            buffer, w_in, (((1,), (1,)), ((), ())), preferred_element_type=jnp.float32
        ).astype(jnp.bfloat16),
        "tp",
        scatter_dimension=0,
        tiled=True,
    ).astype(jnp.float32)
    grad_mixed = (grad_out.astype(jnp.float32) + summed).astype(jnp.bfloat16)
    padded = with_halo(tokens, (("tp", 0),), 3)
    mixed = convolve(padded, kernel, length)
    grad_rows = buffer
    grad_w_in = lax.dot_general(
        lax.all_gather(mixed, "tp", axis=0, tiled=True),
        grad_rows,
        (((0,), (0,)), ((), ())),
        preferred_element_type=jnp.float32,
    )
    grad_pad = with_halo(grad_mixed, (("tp", 0),), 3)
    grad_f = grad_mixed.astype(jnp.float32)
    grad_inputs = grad_f
    taps = []
    for tap in range(KW):
        grad_inputs = grad_inputs + kernel[tap] * grad_pad[6 - tap : 6 - tap + length].astype(
            jnp.float32
        )
        taps.append(jnp.sum(grad_f * padded[tap : tap + length].astype(jnp.float32), axis=0))
    grad_kernel = jnp.stack(taps)
    grad_kernel = lax.psum(grad_kernel, ("dp", "tp"))
    grad_w_in, grad_w_out, grad_bias = (
        lax.psum(grad_w_in.astype(jnp.bfloat16), "dp").astype(jnp.float32),
        lax.psum(grad_w_out.astype(jnp.bfloat16), "dp").astype(jnp.float32),
        lax.psum(grad_bias.astype(jnp.bfloat16), "dp").astype(jnp.float32),
    )
    return (grad_inputs.astype(jnp.bfloat16)[None], grad_w_in, grad_w_out, grad_bias, grad_kernel)


def solution(mesh):
    in_specs = (
        P("dp", "tp", None),
        P("dp", None, "tp"),
        P("dp", "tp", None),
        P(None, "tp"),
        P("tp", None),
        P(),
    )
    out_specs = (P("dp", "tp", None), P(None, "tp"), P("tp", None), P("tp"), P())
    return jax.shard_map(shards, mesh=mesh, in_specs=in_specs, out_specs=out_specs, check_vma=False)
```

profile of v0, /device:TPU:1, one launch (start us, length us, event | category | flops | bytes accessed | tf_op | source)
XLA Modules:
  0.0 317.0 jit_solution(17866380397956469389)
XLA Ops:
  7.2 0.0 copy-start
  7.2 0.0 all-gather.6.cloned.1.call-start
  7.2 0.7 all-gather.6.cloned.1.call-update
  7.9 0.0 all-gather.4.cloned.1.call-start
  8.0 1.0 slice_bitcast_fusion.1
  8.9 4.0 %collective-permute-start.2 = (bf16[3,1280]{1,0:T(4,128)(2,1)S(1)}, bf16[3,1280]{1,0:T(4,128)(2,1)S(1)}, u32[]{:S(2)}, u32[]{:S(2)}) collective-permute-start(bf16[3,1280]{1,0:T(4,128)(2,1)S(1)} %get-tuple-element.27), channel_id=1, source_target_pairs={{0,1},{1,2},{2,3},{4,5},{5,6},{6,7},{8,9},{9,10},{10,11},{12,13},{... | collective-permute-start | bytes 23048 | tf_op jit(solution)/shard_map/ppermute | solution.py:17
  12.9 1.3 collective-permute-start.3
  14.2 1.3 slice_reduce_fusion.6
  15.5 0.0 collective-permute-done.2
  15.5 1.8 collective-permute-done.3
  17.4 4.4 %fusion.52 = bf16[192,1280]{1,0:T(8,128)(2,1)} fusion(bf16[192,1280]{1,0:T(8,128)(2,1)} %bitcast.131, bf16[3,1280]{1,0:T(4,128)(2,1)S(1)} %collective-permute-done.3, bf16[3,1280]{1,0:T(4,128)(2,1)S(1)} %collective-permute-done.2, f32[1280]{0:T(1024)S(1)} %get-tuple-element.20, f32[1280]{0:T(1024)S(1)} %get-tuple-element.21, f32[1280]{0:T(1024)S(1)} %get-tuple-element.16, ...), kind=kLoop, calls=%fused_computation.72 | loop fusion | flops 9830400 | bytes 1034240 | tf_op jit(solution)/shard_map/convert_element_type | solution.py:34
  21.7 0.0 all-gather.4.cloned.1.call-update
  21.8 0.0 all-reduce.3.cloned.1.call-start
  21.8 10.1 %fusion.38 = f32[768,1280]{1,0:T(8,128)} fusion(bf16[1,768,1280]{2,1,0:T(8,128)(2,1)} %param.7), kind=kLoop, calls=%fused_computation.43 | loop fusion | flops 61931520 | bytes 5898240 | tf_op jit(solution)/shard_map/jvp()/erfc | solution.py:27
  31.9 23.0 %all-gather.6.cloned.1.call-done = bf16[1,768,1280]{2,1,0:T(8,128)(2,1)} async-done(((bf16[1,192,1280]{2,1,0:T(8,128)(2,1)}), bf16[1,768,1280]{2,1,0:T(8,128)(2,1)}) %all-gather.6.cloned.1.call-update) | async-done | bytes 1966096 | tf_op jit(solution)/shard_map/all_gather | solution.py:42
  54.9 0.0 copy-start.1
  54.9 0.0 copy-start.4
  54.9 0.0 copy-start.5
  54.9 7.9 %convolution_convert_fusion = bf16[1280,1280]{1,0:T(8,128)(2,1)} fusion(f32[768,1280]{1,0:T(8,128)} %fusion.38, bf16[1,768,1280]{2,1,0:T(8,128)(2,1)} %param.7, bf16[1,768,1280]{2,1,0:T(8,128)(2,1)} %all-gather.6.cloned.1.call-done), kind=kOutput, calls=%fused_computation | convolution fusion | flops 2522152960 | bytes 11141120 | tf_op jit(solution)/shard_map/dot_general | solution.py:50
  62.9 0.0 copy-done
  62.9 0.0 copy-done.1
  62.9 0.0 copy-done.4
  62.9 0.0 copy-done.5
  62.9 4.7 %fusion.80 = (bf16[1280]{0:T(1024)(128)(2,1)S(1)}, bf16[768,1280]{1,0:T(8,128)(2,1)}) fusion(f32[768,1280]{1,0:T(8,128)S(1)} %copy-done.1, bf16[1280,1280]{1,0:T(8,128)(2,1)S(1)} %copy-done, bf16[1,768,1280]{2,1,0:T(8,128)(2,1)S(1)} %copy-done.5, bf16[1,768,1280]{2,1,0:T(8,128)(2,1)S(1)} %copy-done.4), kind=kOutput, calls=%fused_computation.121 | convolution fusion | flops 2532309760 | bytes 13109760 | tf_op jit(solution)/shard_map/dot_general | solution.py:44
  67.6 31.8 %all-gather.4.cloned.1.call-done = bf16[768,1280]{1,0:T(8,128)(2,1)} async-done(((bf16[192,1280]{1,0:T(8,128)(2,1)}), bf16[768,1280]{1,0:T(8,128)(2,1)}) %all-gather.4.cloned.1.call-update) | async-done | bytes 1966096 | tf_op jit(solution)/shard_map/all_gather | solution.py:68
  99.4 6.6 %convolution_convert_fusion.1 = bf16[1280,1280]{1,0:T(8,128)(2,1)} fusion(bf16[768,1280]{1,0:T(8,128)(2,1)} %all-gather.4.cloned.1.call-done, bf16[768,1280]{1,0:T(8,128)(2,1)} %get-tuple-element.30), kind=kOutput, calls=%fused_computation.1 | convolution fusion | flops 2518220800 | bytes 7208960 | tf_op jit(solution)/shard_map/dot_general | solution.py:67
  106.0 0.0 all-reduce.3.cloned.1.call-update
  106.1 0.2 reduce-scatter.2.cloned.1.call-start
  106.3 6.6 %convolution_convert_fusion.2 = bf16[768,1280]{1,0:T(8,128)(2,1)} fusion(bf16[768,1280]{1,0:T(8,128)(2,1)} %get-tuple-element.30, bf16[1280,1280]{1,0:T(8,128)(2,1)} %param.9), kind=kOutput, calls=%fused_computation.44 | convolution fusion | flops 2517565440 | bytes 7208960 | tf_op jit(solution)/shard_map/dot_general | solution.py:56
  112.9 0.0 reduce-scatter.2.cloned.1.call-update
  112.9 12.8 %psum.30 = bf16[1280]{0:T(1024)(128)(2,1)S(1)} all-reduce(bf16[1280]{0:T(1024)(128)(2,1)S(1)} %get-tuple-element.29), channel_id=1, replica_groups=mesh['dp'=8,'tp'=4] {'dp'}, use_global_device_ids=true, to_apply=%region_4.0 | all-reduce | flops 1280 | bytes 5120 | tf_op jit(solution)/shard_map/psum | solution.py:87
  125.7 0.6 convert_element_type.123
  126.3 85.8 %all-reduce.3.cloned.1.call-done = (bf16[1280,1280]{1,0:T(8,128)(2,1)}, bf16[1280,1280]{1,0:T(8,128)(2,1)}) async-done(((bf16[1280,1280]{1,0:T(8,128)(2,1)}, bf16[1280,1280]{1,0:T(8,128)(2,1)}), (bf16[1280,1280]{1,0:T(8,128)(2,1)}, bf16[1280,1280]{1,0:T(8,128)(2,1)})) %all-reduce.3.cloned.1.call-update) | async-done | bytes 6553616 | tf_op jit(solution)/shard_map/psum | solution.py:85
  212.1 0.0 copy-start.2
  212.1 5.4 %convert_element_type.119 = f32[1280,1280]{1,0:T(8,128)} convert(bf16[1280,1280]{1,0:T(8,128)(2,1)} %get-tuple-element.22) | non-fusion elementwise | flops 1638400 | bytes 9830400 | tf_op jit(solution)/shard_map/convert_element_type | solution.py:85
  217.5 0.0 copy-done.2
  217.5 3.3 %convert_element_type.122 = f32[1280,1280]{1,0:T(8,128)} convert(bf16[1280,1280]{1,0:T(8,128)(2,1)S(1)} %copy-done.2) | non-fusion elementwise | flops 1638400 | bytes 9830400 | tf_op jit(solution)/shard_map/convert_element_type | solution.py:86
  220.8 35.1 %reduce-scatter.2.cloned.1.call-done = bf16[192,1280]{1,0:T(8,128)(2,1)} async-done(((bf16[768,1280]{1,0:T(8,128)(2,1)}), bf16[192,1280]{1,0:T(8,128)(2,1)}) %reduce-scatter.2.cloned.1.call-update) | async-done | bytes 491536 | tf_op jit(solution)/shard_map/reduce_scatter | solution.py:55
  255.9 3.8 %fusion.66 = (f32[1280]{0:T(1024)S(1)}, f32[1280]{0:T(1024)S(1)}, f32[1280]{0:T(1024)S(1)}, f32[1280]{0:T(1024)S(1)}, f32[1280]{0:T(1024)S(1)}, /*index=5*/f32[1...) fusion(bf16[3,1280]{1,0:T(4,128)(2,1)S(1)} %collective-permute-done.3, bf16[192,1280]{1,0:T(8,128)(2,1)} %bitcast.132, ...), kind=kLoop, calls=%fused_computation.86 | loop fusion | flops 10804480 | bytes 2508800 | tf_op jit(solution)/shard_map/reduce_sum | solution.py:81
  259.7 0.0 copy-start.3
  259.8 0.7 copy-done.3
  260.5 1.3 collective-permute-start
  261.8 4.0 %collective-permute-start.1 = (bf16[3,1280]{1,0:T(4,128)(2,1)S(1)}, bf16[3,1280]{1,0:T(4,128)(2,1)S(1)}, u32[]{:S(2)}, u32[]{:S(2)}) collective-permute-start(bf16[3,1280]{1,0:T(4,128)(2,1)S(1)} %get-tuple-element.26), channel_id=1, source_target_pairs={{0,1},{1,2},{2,3},{4,5},{5,6},{6,7},{8,9},{9,10},{10,11},{12,13},{... | collective-permute-start | bytes 23048 | tf_op jit(solution)/shard_map/ppermute | solution.py:17
  265.8 0.1 stack.31
  265.8 40.3 %psum.31 = f32[7,1280]{1,0:T(8,128)} all-reduce(f32[7,1280]{1,0:T(8,128)S(1)} %stack.31), channel_id=1, replica_groups=mesh['dp'=8,'tp'=4] {'dp','tp'}, use_global_device_ids=true, to_apply=%region_12.0 | all-reduce | flops 8960 | bytes 71680 | tf_op jit(solution)/shard_map/psum | solution.py:83
  306.2 0.0 collective-permute-done
  306.2 0.0 collective-permute-done.1
  306.2 4.3 %fusion.76 = bf16[1,192,1280]{2,1,0:T(8,128)(2,1)} fusion(bf16[192,1280]{1,0:T(8,128)(2,1)} %copy-done.3, bf16[3,1280]{1,0:T(4,128)(2,1)S(1)} %collective-permute-done.1, f32[1280]{0:T(1024)S(1)} %get-tuple-element.20, f32[1280]{0:T(1024)S(1)} %get-tuple-element.21, f32[1280]{0:T(1024)S(1)} %get-tuple-element.16, f32[1280]{0:T(1024)S(1)} %get-tuple-element.17, ...), kind=kLoop, calls=%fused_computation.109 | loop fusion | flops 9830400 | bytes 1034240 | tf_op jit(solution)/shard_map/broadcast_in_dim | solution.py:89
  (8 shorter events, 0.0 us)
Async XLA Ops:
  7.2 55.7 %copy-start = (bf16[1280,1280]{1,0:T(8,128)(2,1)S(1)}, bf16[1280,1280]{1,0:T(8,128)(2,1)}, u32[]{:S(2)}) copy-start(bf16[1280,1280]{1,0:T(8,128)(2,1)} %param.10) | copy-start | bytes 9830404
  7.2 47.8 %all-gather.6.cloned.1.call-start = ((), (), s32[]{:S(2)}) async-start(), calls=%async_computation.3 | async-start | bytes 2457600 | tf_op jit(solution)/shard_map/all_gather | solution.py:42
  7.9 91.5 %all-gather.4.cloned.1.call-start = ((), (), s32[]{:S(2)}) async-start(), calls=%async_computation.2 | async-start | bytes 2457600 | tf_op jit(solution)/shard_map/all_gather | solution.py:68
  8.9 6.6 %collective-permute-start.2 = (bf16[3,1280]{1,0:T(4,128)(2,1)S(1)}, bf16[3,1280]{1,0:T(4,128)(2,1)S(1)}, u32[]{:S(2)}, u32[]{:S(2)}) collective-permute-start(bf16[3,1280]{1,0:T(4,128)(2,1)S(1)} %get-tuple-element.27), channel_id=1, source_target_pairs={{0,1},{1,2},{2,3},{4,5},{5,6},{6,7},{8,9},{9,10},{10,11},{12,13},{... | collective-permute-start | bytes 23048 | tf_op jit(solution)/shard_map/ppermute | solution.py:17
  12.9 4.4 %collective-permute-start.3 = (bf16[3,1280]{1,0:T(4,128)(2,1)S(1)}, bf16[3,1280]{1,0:T(4,128)(2,1)S(1)}, u32[]{:S(2)}, u32[]{:S(2)}) collective-permute-start(bf16[3,1280]{1,0:T(4,128)(2,1)S(1)} %get-tuple-element.28), channel_id=1, source_target_pairs={{1,0},{2,1},{3,2},{5,4},{6,5},{7,6},{9,8},{10,9},{11,10},{13,12},{... | collective-permute-start | bytes 23048 | tf_op jit(solution)/shard_map/ppermute | solution.py:19
  21.8 190.4 %all-reduce.3.cloned.1.call-start = ((), (), s32[]{:S(2)}) async-start(), calls=%async_computation.4 | async-start | bytes 13107200 | tf_op jit(solution)/shard_map/psum | solution.py:85
  54.9 7.9 %copy-start.1 = (f32[768,1280]{1,0:T(8,128)S(1)}, f32[768,1280]{1,0:T(8,128)}, u32[]{:S(2)}) copy-start(f32[768,1280]{1,0:T(8,128)} %fusion.38) | copy-start | bytes 11796484
  54.9 7.9 %copy-start.4 = (bf16[1,768,1280]{2,1,0:T(8,128)(2,1)S(1)}, bf16[1,768,1280]{2,1,0:T(8,128)(2,1)}, u32[]{:S(2)}) copy-start(bf16[1,768,1280]{2,1,0:T(8,128)(2,1)} %param.7) | copy-start | bytes 5898244
  54.9 7.9 %copy-start.5 = (bf16[1,768,1280]{2,1,0:T(8,128)(2,1)S(1)}, bf16[1,768,1280]{2,1,0:T(8,128)(2,1)}, u32[]{:S(2)}) copy-start(bf16[1,768,1280]{2,1,0:T(8,128)(2,1)} %all-gather.6.cloned.1.call-done) | copy-start | bytes 5898244
  106.1 149.8 %reduce-scatter.2.cloned.1.call-start = ((), (), s32[]{:S(2)}) async-start(), calls=%async_computation.1 | async-start | bytes 2457600 | tf_op jit(solution)/shard_map/reduce_scatter | solution.py:55
  212.1 5.4 %copy-start.2 = (bf16[1280,1280]{1,0:T(8,128)(2,1)S(1)}, bf16[1280,1280]{1,0:T(8,128)(2,1)}, u32[]{:S(2)}) copy-start(bf16[1280,1280]{1,0:T(8,128)(2,1)} %get-tuple-element.23) | copy-start | bytes 9830404
  259.7 0.8 copy-start.3
  260.5 45.7 %collective-permute-start = (bf16[3,1280]{1,0:T(4,128)(2,1)S(1)}, bf16[3,1280]{1,0:T(4,128)(2,1)S(1)}, u32[]{:S(2)}, u32[]{:S(2)}) collective-permute-start(bf16[3,1280]{1,0:T(4,128)(2,1)S(1)} %get-tuple-element.25), channel_id=1, source_target_pairs={{1,0},{2,1},{3,2},{5,4},{6,5},{7,6},{9,8},{10,9},{11,10},{13,12},{... | collective-permute-start | bytes 23048 | tf_op jit(solution)/shard_map/ppermute | solution.py:19
  261.8 44.4 %collective-permute-start.1 = (bf16[3,1280]{1,0:T(4,128)(2,1)S(1)}, bf16[3,1280]{1,0:T(4,128)(2,1)S(1)}, u32[]{:S(2)}, u32[]{:S(2)}) collective-permute-start(bf16[3,1280]{1,0:T(4,128)(2,1)S(1)} %get-tuple-element.26), channel_id=1, source_target_pairs={{0,1},{1,2},{2,3},{4,5},{5,6},{6,7},{8,9},{9,10},{10,11},{12,13},{... | collective-permute-start | bytes 23048 | tf_op jit(solution)/shard_map/ppermute | solution.py:17
Sparse Core Ops, SparseCore 0:
  9.6 45.3 all-gather.5
  57.1 42.3 all-gather.3
  106.2 105.8 all-reduce.2
  214.3 41.5 reduce-scatter.1
where the time goes:
time: 319 us; the launch traced here: 317 us
  waiting for transfers between devices  178 us (56%)
  blocking collectives  53.1 us (17%)
  other arithmetic  31.8 us (10%)
  matrix products  25.8 us (8%)
  between operations  13.9 us (4%)
  starting transfers between devices  10.9 us (3%)
    psum x1, waiting for transfers between devices, shards(): lax.psum(grad_w_in.astype(jnp.bfloat16), 'dp').astype(jnp.float32)  85.8 us
    psum x1, blocking collectives, shards(): grad_kernel = lax.psum(grad_kernel, ('dp', 'tp'))  40.3 us
    reduce_scatter x1, waiting for transfers between devices, shards(): lax.psum_scatter(lax.dot_general(buffer, w_in, (((1,), (1,)), ((), ())),...  35.1 us
    all_gather x1, waiting for transfers between devices, shards(): lax.all_gather(mixed, 'tp', axis=0, tiled=True)  31.8 us
    all_gather x1, waiting for transfers between devices, shards(): piece = lax.all_gather(grad_out, 'tp', axis=0, tiled=True)  23 us
    psum x1, blocking collectives, shards(): lax.psum(grad_bias.astype(jnp.bfloat16), 'dp').astype(jnp.float32)  12.8 us
    another operation x1, other arithmetic, gelu_exact(): return jax.nn.gelu(value, approximate=False)  10.1 us
    ppermute x2, starting transfers between devices, with_halo(): lax.ppermute(tail, axis, [(i, (i + 1) % count) for i in range(ends)])  8.01 us
  transfers between devices with their start and end apart: 8, of which 5 were waited for; matrix products, arithmetic and copies ran while one was open for 14% of the time, Pallas kernels for 0%

commit v1 on v0

v1 whole, which is shorter than its diff:
```python
import functools

import jax
import jax.numpy as jnp
from jax import lax
from jax.experimental import pallas as pl
from jax.experimental.pallas import tpu as pltpu
from jax.sharding import PartitionSpec as P

KW = 7
EDGE = 16
F32 = jnp.float32
BF16 = jnp.bfloat16
MESH = pl.DeviceIdType.MESH


def dot(a, b, dims):
    return lax.dot_general(a, b, (dims, ((), ())), preferred_element_type=F32)


def chunk_of(size):
    return 256 if size % 256 == 0 else size


def body(
    n, dp_size, rows_in, rows_out,
    x_ref, h_ref, up_ref, win_ref, wout_ref, k_ref,
    gin_ref, gwin_ref, gwout_ref, small_ref,
    act, gh, up_all, mix_all, part, zrecv, xpad, gpad, acc_in, acc_out, bias,
    psend_in, psend_out, precv_in, precv_out, rsend_in, rsend_out, rrecv_in, rrecv_out,
    k1, k2,
    hs, hr, us, ur, ms, mr, zs, zr, ps, pr, rs, rr, ds, dr, gs, gr, k1s, k1r, k2s, k2r,
):
    chips = dp_size // 2
    me = lax.axis_index("tp")
    dp = lax.axis_index("dp")
    core = lax.rem(dp, 2)
    chip = dp // 2
    tokens, width = x_ref.shape
    hidden = h_ref.shape[2]
    wide = chunk_of(width)
    tall = chunk_of(hidden)

    def flip(i):
        return jnp.where(i < chips // 2, i, chips // 2 + chips - 1 - i)

    pos = flip(chip)
    spots = (pos, lax.rem(chips - pos, chips))
    after = (
        flip(lax.rem(pos + 1, chips)) * 2 + core,
        flip(lax.rem(pos + chips - 1, chips)) * 2 + core,
    )
    partner = dp + 1 - 2 * core

    barrier = pltpu.get_barrier_semaphore()
    for j in range(1, n):
        pl.semaphore_signal(
            barrier, inc=1, device_id=(dp, lax.rem(me + j, n)), device_id_type=MESH
        )
    for j in range(1, dp_size):
        pl.semaphore_signal(
            barrier, inc=1, device_id=(lax.rem(dp + j, dp_size), me), device_id_type=MESH
        )
    pl.semaphore_wait(barrier, n - 1 + dp_size - 1)

    def send(src, dst, s, r, to):
        return pltpu.make_async_remote_copy(
            src_ref=src, dst_ref=dst, send_sem=s, recv_sem=r, device_id=to, device_id_type=MESH
        )

    pending = []

    def start(cond, make):
        if cond is None:
            make().start()
        else:

            @pl.when(cond)
            def _():
                make().start()

        pending.append((cond, make))

    ways = (0, 1)
    step_of = (1, -1)
    room = (me, n - 1 - me)
    ahead = (n - 1 - me, me)

    def chain(buf, s, r, d, back):
        block = me - step_of[d] * back
        safe = jnp.clip(block, 0, n - 1)
        to = (dp, jnp.clip(me + step_of[d], 0, n - 1))
        return send(buf.at[safe], buf.at[safe], s.at[d, safe], r.at[d, safe], to)

    def edge(src, low, high, s, r, d):
        to = (dp, jnp.clip(me + step_of[d], 0, n - 1))
        if d == 0:
            return send(
                src.at[pl.ds(high, EDGE)], low, s.at[d], r.at[d], to
            )
        return send(src.at[pl.ds(0, EDGE)], low, s.at[d], r.at[d], to)

    def x_edge(d):
        if d == 0:
            return edge(x_ref, xpad.at[pl.ds(0, EDGE)], tokens - EDGE, hs, hr, 0)
        return edge(x_ref, xpad.at[pl.ds(EDGE + tokens, EDGE)], 0, hs, hr, 1)

    def up_first(d):
        to = (dp, jnp.clip(me + step_of[d], 0, n - 1))
        return send(up_ref, up_all.at[me], us.at[d, me], ur.at[d, me], to)

    for d in ways:
        start(ahead[d] > 0, functools.partial(x_edge, d))
    for d in ways:
        start(ahead[d] > 0, functools.partial(up_first, d))

    if act.shape[2] > hidden:
        act[...] = jnp.zeros_like(act)

    def gelu_step(i, _):
        b = i // (tokens // 32)
        at = pl.ds(pl.multiple_of(lax.rem(i, tokens // 32) * 32, 32), 32)
        v = h_ref[b, at, :].astype(F32)
        cdf = 0.5 + 0.5 * lax.erf(v * 0.7071067811865476)
        act[b, at, pl.ds(0, hidden)] = (v * cdf).astype(BF16)
        gh[b, at, :] = (cdf + v * (0.3989422804014327 * jnp.exp(-0.5 * v * v))).astype(BF16)
        return 0

    lax.fori_loop(0, n * (tokens // 32), gelu_step, 0)
    xpad[pl.ds(EDGE, tokens), :] = x_ref[...]

    @pl.when(me == 0)
    def _():
        xpad[pl.ds(0, EDGE), :] = jnp.zeros((EDGE, width), BF16)
        gpad[pl.ds(0, EDGE), :] = jnp.zeros((EDGE, width), BF16)

    @pl.when(me == n - 1)
    def _():
        xpad[pl.ds(EDGE + tokens, EDGE), :] = jnp.zeros((EDGE, width), BF16)
        gpad[pl.ds(EDGE + tokens, EDGE), :] = jnp.zeros((EDGE, width), BF16)

    for d in ways:

        @pl.when(room[d] > 0)
        def _(d=d):
            x_edge(d).wait_recv()

    def mix_step(i, _):
        at = pl.ds(pl.multiple_of(i * 128, 128), 128)
        x = xpad[:, at].astype(F32)
        taps = k_ref[:, at]
        total = x[EDGE : EDGE + tokens]
        for tap in range(KW):
            low = EDGE - 3 + tap
            total = total + taps[tap : tap + 1] * x[low : low + tokens]
        mix_all[me, :, at] = total.astype(BF16)
        return 0

    lax.fori_loop(0, width // 128, mix_step, 0)

    bias[...] = jnp.zeros_like(bias)
    acc_in[...] = jnp.zeros_like(acc_in)
    acc_out[...] = jnp.zeros_like(acc_out)

    def use_upstream(src, b):
        def back_step(i, _):
            at = pl.ds(pl.multiple_of(i * tall, tall), tall) if tall < hidden else pl.ds(0, hidden)
            back = dot(src[...], wout_ref[at, :], ((1,), (1,)))
            grad = (gh[b, :, at].astype(F32) * back).astype(BF16)
            gh[b, :, at] = grad
            bias[:, at] += jnp.sum(grad.astype(F32), axis=0, keepdims=True)
            return 0

        lax.fori_loop(0, hidden // tall, back_step, 0)

        def out_step(i, _):
            at = pl.ds(pl.multiple_of(i * wide, wide), wide)
            acc_out[:, at] += dot(act[b], src[:, at], ((0,), (0,)))
            part[b, :, at] = dot(gh[b], win_ref[at, :], ((1,), (1,))).astype(BF16)
            return 0

        lax.fori_loop(0, width // wide, out_step, 0)

    def use_mixed(b):
        def in_step(i, _):
            at = pl.ds(pl.multiple_of(i * wide, wide), wide)
            acc_in[at, :] += dot(mix_all[b, :, at], gh[b], ((0,), (0,)))
            return 0

        lax.fori_loop(0, width // wide, in_step, 0)

    def mix_chain(d, back):
        return chain(mix_all, ms, mr, d, back)

    def up_chain(d, back):
        return chain(up_all, us, ur, d, back)

    for d in ways:
        start((ahead[d] > 0) & (room[d] == 0), functools.partial(mix_chain, d, 0))
    use_upstream(up_ref, me)
    for back in range(1, n):
        for d in ways:

            @pl.when(room[d] >= back)
            def _(d=d):
                up_chain(d, back).wait_recv()

            start((room[d] >= back) & (ahead[d] > 0), functools.partial(up_chain, d, back))
            start((room[d] == back) & (ahead[d] > 0), functools.partial(mix_chain, d, 0))
        for d in ways:

            @pl.when(room[d] >= back)
            def _(d=d):
                b = jnp.clip(me - step_of[d] * back, 0, n - 1)
                use_upstream(up_all.at[b], b)

    sets = (
        (acc_out, psend_out, precv_out, rsend_out, rrecv_out, gwout_ref, rows_out),
        (acc_in, psend_in, precv_in, rsend_in, rrecv_in, gwin_ref, rows_in),
    )

    def rows_at(w, half, d, block):
        rows = sets[w][6]
        return pl.ds(pl.multiple_of(((half * 2 + d) * chips + block) * rows, 8), rows)

    def pair_copy(w):
        return send(sets[w][1], sets[w][2], ps.at[w], pr.at[w], (partner, me))

    def pair_start(w):
        for d in ways:
            for block in range(chips):
                sets[w][1][d, block] = sets[w][0][rows_at(w, 1 - core, d, block), :].astype(BF16)
        start(None, functools.partial(pair_copy, w))

    def own(w, d, block):
        return sets[w][0][rows_at(w, core, d, block), :] + sets[w][2][d, block].astype(F32)

    def ring_reduce(w, d, s):
        return send(
            sets[w][3].at[d, s], sets[w][4].at[d, s], rs.at[w, d, s], rr.at[w, d, s], (after[d], me)
        )

    def ring_gather(w, d, s):
        block = lax.rem(spots[d] + 1 - s + chips, chips)
        ref = sets[w][5].at[core, d, block]
        at = chips - 1 + s
        return send(ref, ref, rs.at[w, d, at], rr.at[w, d, at], (after[d], me))

    def across(w, d, block, half):
        ref = sets[w][5].at[half, d, block]
        return send(ref, ref, ds.at[w, d, block], dr.at[w, d, block], (partner, me))

    last = 2 * (chips - 1)

    def ring_step(w, s):
        if s > last:
            return
        if s == 0:
            pair_copy(w).wait_recv()
        for d in ways:
            spot = spots[d]
            if s < chips:
                block = lax.rem(spot - s + chips, chips)
                value = own(w, d, block)
                if s > 0:
                    ring_reduce(w, d, s - 1).wait_recv()
                    value = value + sets[w][4][d, s - 1].astype(F32)
                if s < chips - 1:
                    sets[w][3][d, s] = value.astype(BF16)
                    start(None, functools.partial(ring_reduce, w, d, s))
                    continue
                sets[w][5][core, d, block] = value.astype(BF16)
            else:
                block = lax.rem(spot + 1 - (s - chips + 1) + chips, chips)
                ring_arrive(w, d, s - chips).wait_recv()
            if s < last:
                start(None, functools.partial(ring_gather, w, d, s - chips + 1))
            start(None, functools.partial(across, w, d, block, core))

    def ring_arrive(w, d, s):
        block = lax.rem(spots[d] - s + chips, chips)
        ref = sets[w][5].at[core, d, block]
        at = chips - 1 + s
        return send(ref, ref, rs.at[w, d, at], rr.at[w, d, at], (after[d], me))

    def ring_end(w):
        for d in ways:
            for block in range(chips):
                across(w, d, block, 1 - core).wait_recv()

    def target(d, t, behind):
        place = room[d] - behind
        block = n - 1 - t + place
        return block if d == 0 else n - 1 - block

    def z_slot(d, block, owner):
        return jnp.where((block == owner) & (d == 1), n, block)

    def z_send(d, t):
        block = jnp.clip(target(d, t, 0), 0, n - 1)
        to = jnp.clip(me + step_of[d], 0, n - 1)
        return send(
            part.at[block], zrecv.at[z_slot(d, block, to)], zs.at[d, t], zr.at[d, t], (dp, to)
        )

    def z_arrive(d, t):
        block = jnp.clip(target(d, t, 1), 0, n - 1)
        slot = zrecv.at[z_slot(d, block, me)]
        return send(slot, slot, zs.at[d, t], zr.at[d, t], (dp, jnp.clip(me + 1, 0, n - 1)))

    def z_step(t):
        if t > n - 1:
            return
        for d in ways:
            if t > 0:

                @pl.when((room[d] >= 1) & (room[d] - 1 <= t - 1))
                def _(d=d):
                    z_arrive(d, t - 1).wait_recv()
                    if t < n - 1:
                        block = jnp.clip(target(d, t - 1, 1), 0, n - 1)
                        part[block] = (
                            part[block].astype(F32) + zrecv[z_slot(d, block, me)].astype(F32)
                        ).astype(BF16)

            if t < n - 1:
                start((room[d] <= t) & (ahead[d] > 0), functools.partial(z_send, d, t))

    pair_start(0)
    z_step(0)
    use_mixed(me)
    ring_step(0, 0)
    per = -(-last // (n - 1))
    done = 1
    for back in range(1, n):
        for d in ways:

            @pl.when(room[d] >= back)
            def _(d=d):
                mix_chain(d, back).wait_recv()

            start((room[d] >= back) & (ahead[d] > 0), functools.partial(mix_chain, d, back))
        for d in ways:

            @pl.when(room[d] >= back)
            def _(d=d):
                use_mixed(jnp.clip(me - step_of[d] * back, 0, n - 1))

        if back < n - 1:
            z_step(back)
        for _ in range(per):
            if back < n - 1:
                ring_step(0, done)
                done += 1
    pair_start(1)
    while done <= last:
        ring_step(0, done)
        done += 1
    ring_step(1, 0)
    z_step(n - 1)

    def sum_step(i, _):
        at = pl.ds(pl.multiple_of(i * 128, 128), 128)
        total = part[me, :, at].astype(F32)
        left = jnp.where(me > 0, zrecv[me, :, at].astype(F32), 0.0)
        right = jnp.where(me < n - 1, zrecv[n, :, at].astype(F32), 0.0)
        gpad[pl.ds(EDGE, tokens), at] = (
            up_ref[:, at].astype(F32) + (total + left + right)
        ).astype(BF16)
        return 0

    lax.fori_loop(0, width // 128, sum_step, 0)

    def g_edge(d):
        to = (dp, jnp.clip(me + step_of[d], 0, n - 1))
        src = gpad.at[pl.ds(tokens if d == 0 else EDGE, EDGE)]
        dst = gpad.at[pl.ds(0 if d == 0 else EDGE + tokens, EDGE)]
        return send(src, dst, gs.at[d], gr.at[d], to)

    for d in ways:
        start(ahead[d] > 0, functools.partial(g_edge, d))
    ring_step(1, 1)

    def taps_step(i, _):
        at = pl.ds(pl.multiple_of(i * 128, 128), 128)
        g = gpad[pl.ds(EDGE, tokens), at].astype(F32)
        x = xpad[:, at].astype(F32)
        sums = [
            jnp.sum(g * x[EDGE - 3 + tap : EDGE - 3 + tap + tokens], axis=0, keepdims=True)
            for tap in range(KW)
        ]
        sums.append(jnp.zeros_like(sums[0]))
        k1[me, :, at] = jnp.concatenate(sums, axis=0)
        return 0

    lax.fori_loop(0, width // 128, taps_step, 0)

    def k1_send(j):
        to = lax.rem(me + j, n)
        return send(k1.at[me], k1.at[me], k1s.at[j], k1r.at[me], (dp, to))

    def k1_arrive(j):
        src = lax.rem(me + j, n)
        return send(k1.at[src], k1.at[src], k1s.at[j], k1r.at[src], (dp, src))

    for j in range(1, n):
        start(None, functools.partial(k1_send, j))
    for d in ways:

        @pl.when(room[d] > 0)
        def _(d=d):
            g_edge(d).wait_recv()

    def gin_step(i, _):
        at = pl.ds(pl.multiple_of(i * 128, 128), 128)
        g = gpad[:, at].astype(F32)
        taps = k_ref[:, at]
        total = g[EDGE : EDGE + tokens]
        for tap in range(KW):
            low = EDGE + 3 - tap
            total = total + taps[tap : tap + 1] * g[low : low + tokens]
        gin_ref[:, at] = total.astype(BF16)
        return 0

    lax.fori_loop(0, width // 128, gin_step, 0)
    ring_step(1, 2)
    for j in range(1, n):
        k1_arrive(j).wait_recv()
    taps_sum = k1[0]
    for j in range(1, n):
        taps_sum = taps_sum + k1[j]
    k2[dp, pl.ds(0, 8), :] = taps_sum
    k2[dp, pl.ds(8, 8), pl.ds(0, hidden)] = jnp.broadcast_to(bias[...], (8, hidden))
    if hidden < width:
        k2[dp, pl.ds(8, 8), pl.ds(hidden, width - hidden)] = jnp.zeros((8, width - hidden), F32)

    def k2_send(j):
        to = lax.rem(dp + j, dp_size)
        return send(k2.at[dp], k2.at[dp], k2s.at[j], k2r.at[dp], (to, me))

    def k2_arrive(j):
        src = lax.rem(dp + j, dp_size)
        return send(k2.at[src], k2.at[src], k2s.at[j], k2r.at[src], (src, me))

    for j in range(1, dp_size):
        start(None, functools.partial(k2_send, j))
    for s in range(3, last + 1):
        ring_step(1, s)
    for j in range(1, dp_size):
        k2_arrive(j).wait_recv()
    total = k2[0]
    for j in range(1, dp_size):
        total = total + k2[j]
    small_ref[...] = total
    ring_end(0)
    ring_end(1)
    for cond, make in pending:
        if cond is None:
            make().wait_send()
        else:

            @pl.when(cond)
            def _(make=make):
                make().wait_send()


def shards(n, dp_size, inputs, saved_hidden, upstream, w_in, w_out, kernel):
    chips = dp_size // 2
    tokens, width = inputs.shape[1:]
    hidden = w_in.shape[1]
    rows_in = width // (4 * chips)
    rows_out = -(-hidden // (4 * chips * 8)) * 8
    high = rows_out * 4 * chips
    dma = pltpu.SemaphoreType.DMA
    steps = 2 * (chips - 1)
    vmem = pl.BlockSpec(memory_space=pltpu.VMEM)
    shape = jax.ShapeDtypeStruct
    grad_inputs, grad_w_in, grad_w_out, small = pl.pallas_call(
        functools.partial(body, n, dp_size, rows_in, rows_out),
        out_shape=[
            shape((tokens, width), BF16),
            shape((2, 2, chips, rows_in, hidden), BF16),
            shape((2, 2, chips, rows_out, width), BF16),
            shape((16, width), F32),
        ],
        in_specs=[vmem] * 6,
        out_specs=[vmem] * 4,
        scratch_shapes=[
            pltpu.VMEM((n, tokens, high), BF16),
            pltpu.VMEM((n, tokens, hidden), BF16),
            pltpu.VMEM((n, tokens, width), BF16),
            pltpu.VMEM((n, tokens, width), BF16),
            pltpu.VMEM((n, tokens, width), BF16),
            pltpu.VMEM((n + 1, tokens, width), BF16),
            pltpu.VMEM((tokens + 2 * EDGE, width), BF16),
            pltpu.VMEM((tokens + 2 * EDGE, width), BF16),
            pltpu.VMEM((width, hidden), F32),
            pltpu.VMEM((high, width), F32),
            pltpu.VMEM((1, hidden), F32),
            pltpu.VMEM((2, chips, rows_in, hidden), BF16),
            pltpu.VMEM((2, chips, rows_out, width), BF16),
            pltpu.VMEM((2, chips, rows_in, hidden), BF16),
            pltpu.VMEM((2, chips, rows_out, width), BF16),
            pltpu.VMEM((2, chips - 1, rows_in, hidden), BF16),
            pltpu.VMEM((2, chips - 1, rows_out, width), BF16),
            pltpu.VMEM((2, chips - 1, rows_in, hidden), BF16),
            pltpu.VMEM((2, chips - 1, rows_out, width), BF16),
            pltpu.VMEM((n, 8, width), F32),
            pltpu.VMEM((dp_size, 16, width), F32),
            dma((2,)), dma((2,)),
            dma((2, n)), dma((2, n)),
            dma((2, n)), dma((2, n)),
            dma((2, n)), dma((2, n)),
            dma((2,)), dma((2,)),
            dma((2, 2, steps)), dma((2, 2, steps)),
            dma((2, 2, chips)), dma((2, 2, chips)),
            dma((2,)), dma((2,)),
            dma((n,)), dma((n,)),
            dma((dp_size,)), dma((dp_size,)),
        ],
        compiler_params=pltpu.CompilerParams(
            collective_id=0, has_side_effects=True, vmem_limit_bytes=67043328
        ),
    )(
        inputs[0],
        saved_hidden[0].reshape(n, tokens, hidden),
        upstream[0],
        w_in,
        w_out,
        kernel,
    )
    return (
        grad_inputs[None],
        grad_w_in.reshape(width, hidden).astype(F32),
        grad_w_out.reshape(high, width)[:hidden].astype(F32),
        small[8, :hidden],
        small[:KW],
    )


def solution(mesh):
    in_specs = (
        P("dp", "tp", None),
        P("dp", None, "tp"),
        P("dp", "tp", None),
        P(None, "tp"),
        P("tp", None),
        P(),
    )
    out_specs = (P("dp", "tp", None), P(None, "tp"), P("tp", None), P("tp"), P())
    return jax.shard_map(
        functools.partial(shards, mesh.shape["tp"], mesh.shape["dp"]),
        mesh=mesh,
        in_specs=in_specs,
        out_specs=out_specs,
        check_vma=False,
    )
```

time: 319 us -> 153 us (0.48)
  waiting for transfers between devices: 178 us -> 0 us
  Pallas kernels: 0 us -> 139 us
  blocking collectives: 53.1 us -> 0 us
  matrix products: 25.8 us -> 0 us
  other arithmetic: 31.8 us -> 8.94 us
  between operations: 13.9 us -> 0.64 us
  starting transfers between devices: 10.9 us -> 0 us
    pallas_call x0 -> x1, Pallas kernels: none -> 139 us  [shards(): pl.pallas_call(functools.partial(body, n, dp_size, rows_in, rows_out), ou...]
    psum x1 -> x0, waiting for transfers between devices: 85.8 us -> none  [shards(): lax.psum(grad_w_in.astype(jnp.bfloat16), 'dp').astype(jnp.float32)]
    all_gather x2 -> x0, waiting for transfers between devices: 54.9 us -> none  [the longest x1 31.8 us: shards(): lax.all_gather(mixed, 'tp', axis=0, tiled=True)]
    psum x2 -> x0, blocking collectives: 53.1 us -> none  [the longest x1 40.3 us: shards(): grad_kernel = lax.psum(grad_kernel, ('dp', 'tp'))]
    reduce_scatter x1 -> x0, waiting for transfers between devices: 35.1 us -> none  [shards(): lax.psum_scatter(lax.dot_general(buffer, w_in, (((1,), (1,)), ((), ())),...]
    dot_general x4 -> x0, matrix products: 25.8 us -> none  [the longest x1 7.91 us: shards(): lax.dot_general(activated, piece, (((0,), (0,)), ((), ())), preferred_ele...]
    ppermute x4 -> x0, starting transfers between devices: 10.6 us -> none  [the longest x2 8.01 us: with_halo(): lax.ppermute(tail, axis, [(i, (i + 1) % count) for i in range(ends)])]
    another operation x1 -> x0, other arithmetic: 10.1 us -> none  [gelu_exact(): return jax.nn.gelu(value, approximate=False)]
  transfers between devices with their start and end apart: 8 -> 0, of which waited for: 5 -> 0; matrix products, arithmetic and copies ran while one was open for 14% -> 0% of each run, Pallas kernels for 0% -> 0%
where the time goes in v1:
time: 153 us
  Pallas kernels  139 us (91%)
  other arithmetic  8.94 us (6%)
  local copies, waits for them, and re-layouts  3.58 us (2%)
    pallas_call x1, Pallas kernels, shards(): pl.pallas_call(functools.partial(body, n, dp_size, rows_in, rows_out), ou...  139 us
    convert_element_type x1, other arithmetic, shards(): grad_w_out.reshape(high, width)[:hidden].astype(F32)  8.94 us

profile of v1, /device:TPU:1, one launch (start us, length us, event | category | flops | bytes accessed | tf_op | source)
XLA Modules:
  0.0 152.6 jit_solution(16666314948237830515)
XLA Ops:
  0.6 139.4 %shard_map.101 = (bf16[192,1280]{1,0:T(8,128)(2,1)}, bf16[2,2,4,80,1280]{4,3,2,1,0:T(8,128)(2,1)}, bf16[2,2,4,80,1280]{4,3,2,1,0:T(8,128)(2,1)}, f32[16,1280]{1,0:T(8,128)}) custom-call(bf16[192,1280]{1,0:T(8,128)(2,1)} %bitcast.12, bf16[4,192,1280]{2,1,0:T(8,128)(2,1)} %bitcast.10, bf16[192,1280]{1,0:T(8,128)(2,1)} %bitcast.13, bf16[1280,1280]{1,0:T(8,128)(2,1)} %win_ref.1, ...), custom_call_target="tpu_custom_call" | custom-call | tf_op jit(solution)/shard_map/pallas_call | solution.py:478
  140.0 1.4 slice_reduce_fusion
  141.4 1.4 slice.7
  142.8 0.0 copy-start
  142.8 8.9 %bitcast_convert_fusion = (f32[1280,1280]{1,0:T(8,128)}, f32[1280,1280]{1,0:T(8,128)}) fusion(bf16[2,2,4,80,1280]{4,3,2,1,0:T(8,128)(2,1)} %get-tuple-element.11, bf16[2,2,4,80,1280]{4,3,2,1,0:T(8,128)(2,1)} %get-tuple-element.10), kind=kLoop, calls=%fused_computation | loop fusion | flops 3276800 | bytes 19660800 | tf_op jit(solution)/shard_map/convert_element_type | solution.py:535
  151.8 0.0 copy-done
  151.8 0.8 copy.12
Async XLA Ops:
  142.8 8.9 %copy-start = (bf16[192,1280]{1,0:T(8,128)(2,1)S(1)}, bf16[192,1280]{1,0:T(8,128)(2,1)}, u32[]{:S(2)}) copy-start(bf16[192,1280]{1,0:T(8,128)(2,1)} %get-tuple-element.9) | copy-start | bytes 1474564

commit v2 on v1

--- a/solution.py
+++ b/solution.py
@@ -23,22 +23,30 @@
 
 
 def body(
-    n, dp_size, rows_in, rows_out,
-    x_ref, h_ref, up_ref, win_ref, wout_ref, k_ref,
-    gin_ref, gwin_ref, gwout_ref, small_ref,
-    act, gh, up_all, mix_all, part, zrecv, xpad, gpad, acc_in, acc_out, bias,
-    psend_in, psend_out, precv_in, precv_out, rsend_in, rsend_out, rrecv_in, rrecv_out,
-    k1, k2,
-    hs, hr, us, ur, ms, mr, zs, zr, ps, pr, rs, rr, ds, dr, gs, gr, k1s, k1r, k2s, k2r,
+    n, dp_size, rows_in, rows_out, up_parts, mix_parts,
+    x_hbm, h_hbm, up_hbm, win_hbm, wout_hbm, k_ref, gin_ref, small_ref, *refs,
 ):
+    parts = up_parts + mix_parts
+    finals, refs = refs[:parts], refs[parts:]
+    accs, refs = refs[:parts], refs[parts:]
+    psends, refs = refs[:parts], refs[parts:]
+    precvs, refs = refs[:parts], refs[parts:]
+    rsends, refs = refs[:parts], refs[parts:]
+    rrecvs, refs = refs[:parts], refs[parts:]
+    (
+        h_ref, win_ref, wout_ref,
+        act, gh, up_all, mix_all, part, zrecv, xpad, gpad, bias, k1, k2,
+        ls, hl, ul, hs, hr, us, ur, zs, zr, ps, pr, rs, rr, ds, dr, gs, gr, k1s, k1r, k2s, k2r,
+    ) = refs
     chips = dp_size // 2
     me = lax.axis_index("tp")
     dp = lax.axis_index("dp")
     core = lax.rem(dp, 2)
     chip = dp // 2
-    tokens, width = x_ref.shape
+    tokens, width = x_hbm.shape
     hidden = h_ref.shape[2]
-    wide = chunk_of(width)
+    up_wide = width // up_parts
+    mix_wide = width // mix_parts
     tall = chunk_of(hidden)
 
     def flip(i):
@@ -86,48 +94,52 @@
     room = (me, n - 1 - me)
     ahead = (n - 1 - me, me)
 
-    def chain(buf, s, r, d, back):
-        block = me - step_of[d] * back
-        safe = jnp.clip(block, 0, n - 1)
+    loads = [
+        pltpu.make_async_copy(x_hbm, xpad.at[pl.ds(EDGE, tokens)], ls.at[0]),
+        pltpu.make_async_copy(wout_hbm, wout_ref, ls.at[1]),
+        pltpu.make_async_copy(win_hbm, win_ref, ls.at[2]),
+    ]
+
+    def load_hidden(j):
+        b = lax.rem(me + j, n)
+        return pltpu.make_async_copy(h_hbm.at[b], h_ref.at[b], hl.at[b])
+
+    def load_up(c):
+        src = up_hbm.at[:, pl.ds(c * up_wide, up_wide)]
+        return pltpu.make_async_copy(src, up_all.at[c, me], ul.at[c])
+
+    def place(k, b):
+        return up_all.at[k, b] if k < up_parts else mix_all.at[k - up_parts, b]
+
+    def chain(k, d, back):
+        b = jnp.clip(me - step_of[d] * back, 0, n - 1)
         to = (dp, jnp.clip(me + step_of[d], 0, n - 1))
-        return send(buf.at[safe], buf.at[safe], s.at[d, safe], r.at[d, safe], to)
-
-    def edge(src, low, high, s, r, d):
+        src = place(k, b)
+        if back == 0 and k < up_parts:
+            src = up_hbm.at[:, pl.ds(k * up_wide, up_wide)]
+        return send(src, place(k, b), us.at[k, d, b], ur.at[k, d, b], to)
+
+    def x_edge(d):
         to = (dp, jnp.clip(me + step_of[d], 0, n - 1))
-        if d == 0:
-            return send(
-                src.at[pl.ds(high, EDGE)], low, s.at[d], r.at[d], to
-            )
-        return send(src.at[pl.ds(0, EDGE)], low, s.at[d], r.at[d], to)
-
-    def x_edge(d):
-        if d == 0:
-            return edge(x_ref, xpad.at[pl.ds(0, EDGE)], tokens - EDGE, hs, hr, 0)
-        return edge(x_ref, xpad.at[pl.ds(EDGE + tokens, EDGE)], 0, hs, hr, 1)
-
-    def up_first(d):
-        to = (dp, jnp.clip(me + step_of[d], 0, n - 1))
-        return send(up_ref, up_all.at[me], us.at[d, me], ur.at[d, me], to)
-
+        src = x_hbm.at[pl.ds(tokens - EDGE if d == 0 else 0, EDGE)]
+        dst = xpad.at[pl.ds(0 if d == 0 else EDGE + tokens, EDGE)]
+        return send(src, dst, hs.at[d], hr.at[d], to)
+
+    for d in ways:
+        start(ahead[d] > 0, functools.partial(chain, 0, d, 0))
     for d in ways:
         start(ahead[d] > 0, functools.partial(x_edge, d))
-    for d in ways:
-        start(ahead[d] > 0, functools.partial(up_first, d))
+    load_hidden(0).start()
+    for c in range(up_parts):
+        load_up(c).start()
+    for load in loads:
+        load.start()
+    for j in range(1, n):
+        load_hidden(j).start()
 
     if act.shape[2] > hidden:
         act[...] = jnp.zeros_like(act)
-
-    def gelu_step(i, _):
-        b = i // (tokens // 32)
-        at = pl.ds(pl.multiple_of(lax.rem(i, tokens // 32) * 32, 32), 32)
-        v = h_ref[b, at, :].astype(F32)
-        cdf = 0.5 + 0.5 * lax.erf(v * 0.7071067811865476)
-        act[b, at, pl.ds(0, hidden)] = (v * cdf).astype(BF16)
-        gh[b, at, :] = (cdf + v * (0.3989422804014327 * jnp.exp(-0.5 * v * v))).astype(BF16)
-        return 0
-
-    lax.fori_loop(0, n * (tokens // 32), gelu_step, 0)
-    xpad[pl.ds(EDGE, tokens), :] = x_ref[...]
+    bias[...] = jnp.zeros_like(bias)
 
     @pl.when(me == 0)
     def _():
@@ -139,33 +151,58 @@
         xpad[pl.ds(EDGE + tokens, EDGE), :] = jnp.zeros((EDGE, width), BF16)
         gpad[pl.ds(EDGE + tokens, EDGE), :] = jnp.zeros((EDGE, width), BF16)
 
-    for d in ways:
-
-        @pl.when(room[d] > 0)
-        def _(d=d):
-            x_edge(d).wait_recv()
-
-    def mix_step(i, _):
-        at = pl.ds(pl.multiple_of(i * 128, 128), 128)
-        x = xpad[:, at].astype(F32)
-        taps = k_ref[:, at]
-        total = x[EDGE : EDGE + tokens]
-        for tap in range(KW):
-            low = EDGE - 3 + tap
-            total = total + taps[tap : tap + 1] * x[low : low + tokens]
-        mix_all[me, :, at] = total.astype(BF16)
-        return 0
-
-    lax.fori_loop(0, width // 128, mix_step, 0)
-
-    bias[...] = jnp.zeros_like(bias)
-    acc_in[...] = jnp.zeros_like(acc_in)
-    acc_out[...] = jnp.zeros_like(acc_out)
-
-    def use_upstream(src, b):
+    def gelu(b):
+        pltpu.make_async_copy(h_hbm.at[b], h_ref.at[b], hl.at[b]).wait()
+
+        def gelu_step(i, _):
+            at = pl.ds(pl.multiple_of(i * 32, 32), 32)
+            v = h_ref[b, at, :].astype(F32)
+            cdf = 0.5 + 0.5 * lax.erf(v * 0.7071067811865476)
+            act[b, at, pl.ds(0, hidden)] = (v * cdf).astype(BF16)
+            gh[b, at, :] = (cdf + v * (0.3989422804014327 * jnp.exp(-0.5 * v * v))).astype(BF16)
+            return 0
+
+        lax.fori_loop(0, tokens // 32, gelu_step, 0)
+
+    def mix():
+        def mix_step(i, _):
+            at = pl.ds(pl.multiple_of(i * 128, 128), 128)
+            x = xpad[:, at].astype(F32)
+            taps = k_ref[:, at]
+            total = x[EDGE : EDGE + tokens]
+            for tap in range(KW):
+                low = EDGE - 3 + tap
+                total = total + taps[tap : tap + 1] * x[low : low + tokens]
+            c = i // (mix_wide // 128)
+            lane = pl.ds(pl.multiple_of(lax.rem(i, mix_wide // 128) * 128, 128), 128)
+            mix_all[c, me, :, lane] = total.astype(BF16)
+            return 0
+
+        lax.fori_loop(0, width // 128, mix_step, 0)
+
+    def add_to(acc, at, value, first):
+        if first:
+            acc[at] = value
+        else:
+            acc[at] += value
+
+    def out_dot(c, b, first):
+        def out_step(i, _):
+            at = pl.ds(pl.multiple_of(i * 128, 128), 128)
+            value = dot(act[b], up_all[c, b, :, at], ((0,), (0,)))
+            add_to(accs[c], (slice(None), at), value, first)
+            return 0
+
+        lax.fori_loop(0, up_wide // 128, out_step, 0)
+
+    def back_dot(b):
         def back_step(i, _):
             at = pl.ds(pl.multiple_of(i * tall, tall), tall) if tall < hidden else pl.ds(0, hidden)
-            back = dot(src[...], wout_ref[at, :], ((1,), (1,)))
+            back = None
+            for c in range(up_parts):
+                cols = pl.ds(c * up_wide, up_wide)
+                term = dot(up_all[c, b], wout_ref[at, cols], ((1,), (1,)))
+                back = term if back is None else back + term
             grad = (gh[b, :, at].astype(F32) * back).astype(BF16)
             gh[b, :, at] = grad
             bias[:, at] += jnp.sum(grad.astype(F32), axis=0, keepdims=True)
@@ -173,51 +210,38 @@
 
         lax.fori_loop(0, hidden // tall, back_step, 0)
 
-        def out_step(i, _):
+        wide = chunk_of(width)
+
+        def part_step(i, _):
             at = pl.ds(pl.multiple_of(i * wide, wide), wide)
-            acc_out[:, at] += dot(act[b], src[:, at], ((0,), (0,)))
             part[b, :, at] = dot(gh[b], win_ref[at, :], ((1,), (1,))).astype(BF16)
             return 0
 
-        lax.fori_loop(0, width // wide, out_step, 0)
-
-    def use_mixed(b):
+        lax.fori_loop(0, width // wide, part_step, 0)
+
+    def in_dot(c, b, first):
         def in_step(i, _):
-            at = pl.ds(pl.multiple_of(i * wide, wide), wide)
-            acc_in[at, :] += dot(mix_all[b, :, at], gh[b], ((0,), (0,)))
+            at = pl.ds(pl.multiple_of(i * 128, 128), 128)
+            value = dot(mix_all[c, b, :, at], gh[b], ((0,), (0,)))
+            add_to(accs[up_parts + c], (at, slice(None)), value, first)
             return 0
 
-        lax.fori_loop(0, width // wide, in_step, 0)
-
-    def mix_chain(d, back):
-        return chain(mix_all, ms, mr, d, back)
-
-    def up_chain(d, back):
-        return chain(up_all, us, ur, d, back)
-
-    for d in ways:
-        start((ahead[d] > 0) & (room[d] == 0), functools.partial(mix_chain, d, 0))
-    use_upstream(up_ref, me)
-    for back in range(1, n):
-        for d in ways:
-
-            @pl.when(room[d] >= back)
-            def _(d=d):
-                up_chain(d, back).wait_recv()
-
-            start((room[d] >= back) & (ahead[d] > 0), functools.partial(up_chain, d, back))
-            start((room[d] == back) & (ahead[d] > 0), functools.partial(mix_chain, d, 0))
-        for d in ways:
-
-            @pl.when(room[d] >= back)
-            def _(d=d):
-                b = jnp.clip(me - step_of[d] * back, 0, n - 1)
-                use_upstream(up_all.at[b], b)
-
-    sets = (
-        (acc_out, psend_out, precv_out, rsend_out, rrecv_out, gwout_ref, rows_out),
-        (acc_in, psend_in, precv_in, rsend_in, rrecv_in, gwin_ref, rows_in),
-    )
+        lax.fori_loop(0, mix_wide // 128, in_step, 0)
+
+    def use(k, b, first=False):
+        if k < up_parts:
+            if k == 0:
+                gelu(b)
+            out_dot(k, b, first)
+            if k == up_parts - 1:
+                back_dot(b)
+        else:
+            in_dot(k - up_parts, b, first)
+
+    sets = [
+        (accs[w], psends[w], precvs[w], rsends[w], rrecvs[w], finals[w], rows_out if w < up_parts else rows_in)
+        for w in range(parts)
+    ]
 
     def rows_at(w, half, d, block):
         rows = sets[w][6]
@@ -326,38 +350,74 @@
             if t < n - 1:
                 start((room[d] <= t) & (ahead[d] > 0), functools.partial(z_send, d, t))
 
-    pair_start(0)
-    z_step(0)
-    use_mixed(me)
-    ring_step(0, 0)
-    per = -(-last // (n - 1))
-    done = 1
-    for back in range(1, n):
-        for d in ways:
-
-            @pl.when(room[d] >= back)
-            def _(d=d):
-                mix_chain(d, back).wait_recv()
-
-            start((room[d] >= back) & (ahead[d] > 0), functools.partial(mix_chain, d, back))
-        for d in ways:
-
-            @pl.when(room[d] >= back)
-            def _(d=d):
-                use_mixed(jnp.clip(me - step_of[d] * back, 0, n - 1))
-
-        if back < n - 1:
-            z_step(back)
-        for _ in range(per):
-            if back < n - 1:
-                ring_step(0, done)
-                done += 1
-    pair_start(1)
-    while done <= last:
-        ring_step(0, done)
-        done += 1
-    ring_step(1, 0)
+    active = []
+
+    def tick():
+        for item in list(active):
+            ring_step(item[0], item[1])
+            item[1] += 1
+            if item[1] > last:
+                active.remove(item)
+
+    for k in range(parts):
+        follow = k + 1
+        if follow < parts and follow != up_parts:
+            for d in ways:
+                start((ahead[d] > 0) & (room[d] == 0), functools.partial(chain, follow, d, 0))
+        if k == 0:
+            load_up(0).wait()
+        use_own = functools.partial(use, k, me, True)
+        if k == up_parts - 1:
+            if k > 0:
+                load_up(k).wait()
+            loads[1].wait()
+            loads[2].wait()
+        use_own()
+        if k == 0:
+            loads[0].wait()
+            for d in ways:
+
+                @pl.when(room[d] > 0)
+                def _(d=d):
+                    x_edge(d).wait_recv()
+
+            mix()
+        if follow == up_parts:
+            for d in ways:
+                start((ahead[d] > 0) & (room[d] == 0), functools.partial(chain, follow, d, 0))
+        for back in range(1, n):
+            for d in ways:
+
+                @pl.when(room[d] >= back)
+                def _(d=d):
+                    chain(k, d, back).wait_recv()
+
+                start((room[d] >= back) & (ahead[d] > 0), functools.partial(chain, k, d, back))
+                if follow < parts:
+                    start((room[d] == back) & (ahead[d] > 0), functools.partial(chain, follow, d, 0))
+            for d in ways:
+
+                @pl.when(room[d] >= back)
+                def _(d=d):
+                    use(k, jnp.clip(me - step_of[d] * back, 0, n - 1))
+
+            tick()
+        pair_start(k)
+        active.append([k, 0])
+        if k >= up_parts - 1:
+            z_step(k - up_parts + 1)
+    for t in range(mix_parts + 1, n - 1):
+        z_step(t)
+        tick()
+    tick()
+    tick()
+    tick()
     z_step(n - 1)
+
+    def own_up(i):
+        c = i // (up_wide // 128)
+        lane = pl.ds(pl.multiple_of(lax.rem(i, up_wide // 128) * 128, 128), 128)
+        return up_all[c, me, :, lane].astype(F32)
 
     def sum_step(i, _):
         at = pl.ds(pl.multiple_of(i * 128, 128), 128)
@@ -365,7 +425,7 @@
         left = jnp.where(me > 0, zrecv[me, :, at].astype(F32), 0.0)
         right = jnp.where(me < n - 1, zrecv[n, :, at].astype(F32), 0.0)
         gpad[pl.ds(EDGE, tokens), at] = (
-            up_ref[:, at].astype(F32) + (total + left + right)
+            own_up(i) + (total + left + right)
         ).astype(BF16)
         return 0
 
@@ -379,7 +439,7 @@
 
     for d in ways:
         start(ahead[d] > 0, functools.partial(g_edge, d))
-    ring_step(1, 1)
+    tick()
 
     def taps_step(i, _):
         at = pl.ds(pl.multiple_of(i * 128, 128), 128)
@@ -423,7 +483,7 @@
         return 0
 
     lax.fori_loop(0, width // 128, gin_step, 0)
-    ring_step(1, 2)
+    tick()
     for j in range(1, n):
         k1_arrive(j).wait_recv()
     taps_sum = k1[0]
@@ -444,16 +504,16 @@
 
     for j in range(1, dp_size):
         start(None, functools.partial(k2_send, j))
-    for s in range(3, last + 1):
-        ring_step(1, s)
+    while active:
+        tick()
     for j in range(1, dp_size):
         k2_arrive(j).wait_recv()
     total = k2[0]
     for j in range(1, dp_size):
         total = total + k2[j]
     small_ref[...] = total
-    ring_end(0)
-    ring_end(1)
+    for w in range(parts):
+        ring_end(w)
     for cond, make in pending:
         if cond is None:
             make().wait_send()
@@ -468,52 +528,49 @@
     chips = dp_size // 2
     tokens, width = inputs.shape[1:]
     hidden = w_in.shape[1]
-    rows_in = width // (4 * chips)
+    up_parts = 2 if width % 256 == 0 else 1
+    mix_parts = 2 if width % (8 * chips * 8) == 0 and width % 256 == 0 else 1
+    parts = up_parts + mix_parts
+    rows_in = width // (4 * chips * mix_parts)
     rows_out = -(-hidden // (4 * chips * 8)) * 8
     high = rows_out * 4 * chips
     dma = pltpu.SemaphoreType.DMA
     steps = 2 * (chips - 1)
     vmem = pl.BlockSpec(memory_space=pltpu.VMEM)
+    hbm = pl.BlockSpec(memory_space=pl.ANY)
     shape = jax.ShapeDtypeStruct
-    grad_inputs, grad_w_in, grad_w_out, small = pl.pallas_call(
-        functools.partial(body, n, dp_size, rows_in, rows_out),
-        out_shape=[
-            shape((tokens, width), BF16),
-            shape((2, 2, chips, rows_in, hidden), BF16),
-            shape((2, 2, chips, rows_out, width), BF16),
-            shape((16, width), F32),
-        ],
-        in_specs=[vmem] * 6,
-        out_specs=[vmem] * 4,
-        scratch_shapes=[
+    sizes = [(rows_out, width // up_parts)] * up_parts + [(rows_in, hidden)] * mix_parts
+    grad_inputs, small, *finals = pl.pallas_call(
+        functools.partial(body, n, dp_size, rows_in, rows_out, up_parts, mix_parts),
+        out_shape=[shape((tokens, width), BF16), shape((16, width), F32)]
+        + [shape((2, 2, chips) + size, BF16) for size in sizes],
+        in_specs=[hbm] * 5 + [vmem],
+        out_specs=[vmem] * (2 + parts),
+        scratch_shapes=[pltpu.VMEM((4 * chips * r, c), F32) for r, c in sizes]
+        + [pltpu.VMEM((2, chips) + size, BF16) for size in sizes] * 2
+        + [pltpu.VMEM((2, chips - 1) + size, BF16) for size in sizes] * 2
+        + [
+            pltpu.VMEM((n, tokens, hidden), BF16),
+            pltpu.VMEM((width, hidden), BF16),
+            pltpu.VMEM((hidden, width), BF16),
             pltpu.VMEM((n, tokens, high), BF16),
             pltpu.VMEM((n, tokens, hidden), BF16),
-            pltpu.VMEM((n, tokens, width), BF16),
-            pltpu.VMEM((n, tokens, width), BF16),
+            pltpu.VMEM((up_parts, n, tokens, width // up_parts), BF16),
+            pltpu.VMEM((mix_parts, n, tokens, width // mix_parts), BF16),
             pltpu.VMEM((n, tokens, width), BF16),
             pltpu.VMEM((n + 1, tokens, width), BF16),
             pltpu.VMEM((tokens + 2 * EDGE, width), BF16),
             pltpu.VMEM((tokens + 2 * EDGE, width), BF16),
-            pltpu.VMEM((width, hidden), F32),
-            pltpu.VMEM((high, width), F32),
             pltpu.VMEM((1, hidden), F32),
-            pltpu.VMEM((2, chips, rows_in, hidden), BF16),
-            pltpu.VMEM((2, chips, rows_out, width), BF16),
-            pltpu.VMEM((2, chips, rows_in, hidden), BF16),
-            pltpu.VMEM((2, chips, rows_out, width), BF16),
-            pltpu.VMEM((2, chips - 1, rows_in, hidden), BF16),
-            pltpu.VMEM((2, chips - 1, rows_out, width), BF16),
-            pltpu.VMEM((2, chips - 1, rows_in, hidden), BF16),
-            pltpu.VMEM((2, chips - 1, rows_out, width), BF16),
             pltpu.VMEM((n, 8, width), F32),
             pltpu.VMEM((dp_size, 16, width), F32),
+            dma((3,)), dma((n,)), dma((up_parts,)),
             dma((2,)), dma((2,)),
+            dma((parts, 2, n)), dma((parts, 2, n)),
             dma((2, n)), dma((2, n)),
-            dma((2, n)), dma((2, n)),
-            dma((2, n)), dma((2, n)),
-            dma((2,)), dma((2,)),
-            dma((2, 2, steps)), dma((2, 2, steps)),
-            dma((2, 2, chips)), dma((2, 2, chips)),
+            dma((parts,)), dma((parts,)),
+            dma((parts, 2, steps)), dma((parts, 2, steps)),
+            dma((parts, 2, chips)), dma((parts, 2, chips)),
             dma((2,)), dma((2,)),
             dma((n,)), dma((n,)),
             dma((dp_size,)), dma((dp_size,)),
@@ -529,10 +586,12 @@
         w_out,
         kernel,
     )
+    columns = [f.reshape(high, width // up_parts)[:hidden] for f in finals[:up_parts]]
+    rows = [f.reshape(width // mix_parts, hidden) for f in finals[up_parts:]]
     return (
         grad_inputs[None],
-        grad_w_in.reshape(width, hidden).astype(F32),
-        grad_w_out.reshape(high, width)[:hidden].astype(F32),
+        jnp.concatenate(rows, axis=0).astype(F32),
+        jnp.concatenate(columns, axis=1).astype(F32),
         small[8, :hidden],
         small[:KW],
     )

time: 153 us -> 146 us (0.954)
  Pallas kernels: 139 us -> 132 us
    pallas_call x1, Pallas kernels: 139 us -> 132 us  [shards(): pl.pallas_call(functools.partial(body, n, dp_size, rows_in, rows_out, up_...]
where the time goes in v2:
time: 146 us; the launch traced here: 145 us
  Pallas kernels  132 us (90%)
  other arithmetic  8.91 us (6%)
  local copies, waits for them, and re-layouts  3.58 us (2%)
    pallas_call x1, Pallas kernels, shards(): pl.pallas_call(functools.partial(body, n, dp_size, rows_in, rows_out, up_...  132 us
    convert_element_type x1, other arithmetic, shards(): jnp.concatenate(rows, axis=0).astype(F32)  8.91 us

profile of v2, /device:TPU:1, one launch (start us, length us, event | category | flops | bytes accessed | tf_op | source)
XLA Modules:
  0.0 145.3 jit_solution(3294825536696057942)
XLA Ops:
  0.6 132.2 %shard_map.101 = (bf16[192,1280]{1,0:T(8,128)(2,1)}, f32[16,1280]{1,0:T(8,128)}, bf16[2,2,4,80,640]{4,3,2,1,0:T(8,128)(2,1)}, bf16[2,2,4,80,640]{4,3,2,1,0:T(8,1...) custom-call(bf16[192,1280]{1,0:T(8,128)(2,1)} %bitcast.14, ...), custom_call_target="tpu_custom_call" | custom-call | tf_op jit(solution)/shard_map/pallas_call | solution.py:543
  132.8 1.4 slice_reduce_fusion
  134.2 1.4 slice.7
  135.6 0.0 copy-start
  135.6 8.9 %maximum_convert_fusion = (f32[1280,1280]{1,0:T(8,128)}, f32[1280,1280]{1,0:T(8,128)}) fusion(bf16[640,1280]{1,0:T(8,128)(2,1)} %bitcast.12, bf16[640,1280]{1,0:T(8,128)(2,1)} %bitcast.11, bf16[1280,640]{1,0:T(8,128)(2,1)} %bitcast.10, bf16[1280,640]{1,0:T(8,128)(2,1)} %bitcast.9), kind=kLoop, calls=%fused_computation | loop fusion | flops 13107200 | bytes 19660800 | tf_op jit(solution)/shard_map/convert_element_type | solution.py:593
  144.5 0.0 copy-done
  144.5 0.8 copy.12
Async XLA Ops:
  135.6 8.9 %copy-start = (bf16[192,1280]{1,0:T(8,128)(2,1)S(1)}, bf16[192,1280]{1,0:T(8,128)(2,1)}, u32[]{:S(2)}) copy-start(bf16[192,1280]{1,0:T(8,128)(2,1)} %get-tuple-element.11) | copy-start | bytes 1474564

commit v3 on v2

--- a/solution.py
+++ b/solution.py
@@ -24,7 +24,7 @@
 
 def body(
     n, dp_size, rows_in, rows_out, up_parts, mix_parts,
-    x_hbm, h_hbm, up_hbm, win_hbm, wout_hbm, k_ref, gin_ref, small_ref, *refs,
+    x_hbm, h_hbm, up_hbm, win_hbm, wout_hbm, k_ref, gin_ref, gk_ref, gb_ref, *refs,
 ):
     parts = up_parts + mix_parts
     finals, refs = refs[:parts], refs[parts:]
@@ -49,15 +49,26 @@
     mix_wide = width // mix_parts
     tall = chunk_of(hidden)
 
-    def flip(i):
-        return jnp.where(i < chips // 2, i, chips // 2 + chips - 1 - i)
-
-    pos = flip(chip)
-    spots = (pos, lax.rem(chips - pos, chips))
-    after = (
-        flip(lax.rem(pos + 1, chips)) * 2 + core,
-        flip(lax.rem(pos + chips - 1, chips)) * 2 + core,
-    )
+    bits = chips.bit_length() - 1
+
+    def mirror(i):
+        return sum((i // 2**p) % 2 * 2 ** (bits - 1 - p) for p in range(bits))
+
+    spots = (chip, mirror(chip))
+    halves = [chips >> (s + 1) for s in range(bits)]
+    starts = [sum(halves[:s]) for s in range(bits)]
+
+    def span(d, s, other):
+        h = halves[s]
+        side = lax.rem(spots[d] // h, 2)
+        low = spots[d] // h * h
+        return low + (h - 2 * h * side if other else 0)
+
+    def peer(d, s):
+        h = halves[s]
+        spot = spots[d] + h - 2 * h * lax.rem(spots[d] // h, 2)
+        return (mirror(spot) if d else spot) * 2 + core
+
     partner = dp + 1 - 2 * core
 
     barrier = pltpu.get_barrier_semaphore()
@@ -125,8 +136,9 @@
         dst = xpad.at[pl.ds(0 if d == 0 else EDGE + tokens, EDGE)]
         return send(src, dst, hs.at[d], hr.at[d], to)
 
-    for d in ways:
-        start(ahead[d] > 0, functools.partial(chain, 0, d, 0))
+    for k in range(2):
+        for d in ways:
+            start(ahead[d] > 0, functools.partial(chain, k, d, 0))
     for d in ways:
         start(ahead[d] > 0, functools.partial(x_edge, d))
     load_hidden(0).start()
@@ -260,57 +272,66 @@
         return sets[w][0][rows_at(w, core, d, block), :] + sets[w][2][d, block].astype(F32)
 
     def ring_reduce(w, d, s):
+        at = pl.ds(starts[s], halves[s])
         return send(
-            sets[w][3].at[d, s], sets[w][4].at[d, s], rs.at[w, d, s], rr.at[w, d, s], (after[d], me)
+            sets[w][3].at[d, at], sets[w][4].at[d, at], rs.at[w, d, s], rr.at[w, d, s],
+            (peer(d, s), me),
         )
 
-    def ring_gather(w, d, s):
-        block = lax.rem(spots[d] + 1 - s + chips, chips)
-        ref = sets[w][5].at[core, d, block]
-        at = chips - 1 + s
-        return send(ref, ref, rs.at[w, d, at], rr.at[w, d, at], (after[d], me))
-
-    def across(w, d, block, half):
-        ref = sets[w][5].at[half, d, block]
-        return send(ref, ref, ds.at[w, d, block], dr.at[w, d, block], (partner, me))
-
-    last = 2 * (chips - 1)
+    def ring_gather(w, d, s, other):
+        ref = sets[w][5].at[core, d, pl.ds(span(d, s, other), halves[s])]
+        at = 2 * bits - 1 - s
+        return send(ref, ref, rs.at[w, d, at], rr.at[w, d, at], (peer(d, s), me))
+
+    def across(w, d, s, half):
+        if s == bits:
+            ref = sets[w][5].at[half, d, pl.ds(spots[d], 1)]
+        else:
+            ref = sets[w][5].at[half, d, pl.ds(span(d, s, True), halves[s])]
+        return send(ref, ref, ds.at[w, d, s], dr.at[w, d, s], (partner, me))
+
+    last = 2 * bits
 
     def ring_step(w, s):
-        if s > last:
-            return
+        acc, _, _, rsend, rrecv, final, _ = sets[w]
         if s == 0:
             pair_copy(w).wait_recv()
         for d in ways:
-            spot = spots[d]
-            if s < chips:
-                block = lax.rem(spot - s + chips, chips)
-                value = own(w, d, block)
+            if s <= bits:
                 if s > 0:
                     ring_reduce(w, d, s - 1).wait_recv()
-                    value = value + sets[w][4][d, s - 1].astype(F32)
-                if s < chips - 1:
-                    sets[w][3][d, s] = value.astype(BF16)
-                    start(None, functools.partial(ring_reduce, w, d, s))
+
+                def value(block, s=s, d=d):
+                    if s == 0:
+                        return own(w, d, block)
+                    got = rrecv[d, starts[s - 1] + block - span(d, s - 1, False)].astype(F32)
+                    if s == 1:
+                        return own(w, d, block) + got
+                    return acc[rows_at(w, core, d, block), :] + got
+
+                if s == bits:
+                    final[core, d, spots[d]] = value(spots[d]).astype(BF16)
+                    start(None, functools.partial(ring_gather, w, d, s - 1, False))
+                    start(None, functools.partial(across, w, d, bits, core))
                     continue
-                sets[w][5][core, d, block] = value.astype(BF16)
+                for j in range(halves[s]):
+                    rsend[d, starts[s] + j] = value(span(d, s, True) + j).astype(BF16)
+                start(None, functools.partial(ring_reduce, w, d, s))
+                if s > 0:
+                    for j in range(halves[s]):
+                        block = span(d, s, False) + j
+                        acc[rows_at(w, core, d, block), :] = value(block)
             else:
-                block = lax.rem(spot + 1 - (s - chips + 1) + chips, chips)
-                ring_arrive(w, d, s - chips).wait_recv()
-            if s < last:
-                start(None, functools.partial(ring_gather, w, d, s - chips + 1))
-            start(None, functools.partial(across, w, d, block, core))
-
-    def ring_arrive(w, d, s):
-        block = lax.rem(spots[d] - s + chips, chips)
-        ref = sets[w][5].at[core, d, block]
-        at = chips - 1 + s
-        return send(ref, ref, rs.at[w, d, at], rr.at[w, d, at], (after[d], me))
+                step = 2 * bits - s
+                ring_gather(w, d, step, True).wait_recv()
+                if step > 0:
+                    start(None, functools.partial(ring_gather, w, d, step - 1, False))
+                start(None, functools.partial(across, w, d, step, core))
 
     def ring_end(w):
         for d in ways:
-            for block in range(chips):
-                across(w, d, block, 1 - core).wait_recv()
+            for s in range(bits + 1):
+                across(w, d, s, 1 - core).wait_recv()
 
     def target(d, t, behind):
         place = room[d] - behind
@@ -360,10 +381,7 @@
                 active.remove(item)
 
     for k in range(parts):
-        follow = k + 1
-        if follow < parts and follow != up_parts:
-            for d in ways:
-                start((ahead[d] > 0) & (room[d] == 0), functools.partial(chain, follow, d, 0))
+        follow = k + 2
         if k == 0:
             load_up(0).wait()
         use_own = functools.partial(use, k, me, True)
@@ -382,7 +400,7 @@
                     x_edge(d).wait_recv()
 
             mix()
-        if follow == up_parts:
+        if follow < parts:
             for d in ways:
                 start((ahead[d] > 0) & (room[d] == 0), functools.partial(chain, follow, d, 0))
         for back in range(1, n):
@@ -511,7 +529,8 @@
     total = k2[0]
     for j in range(1, dp_size):
         total = total + k2[j]
-    small_ref[...] = total
+    gk_ref[...] = total[:KW]
+    gb_ref[...] = total[8:9, :hidden]
     for w in range(parts):
         ring_end(w)
     for cond, make in pending:
@@ -528,24 +547,24 @@
     chips = dp_size // 2
     tokens, width = inputs.shape[1:]
     hidden = w_in.shape[1]
-    up_parts = 2 if width % 256 == 0 else 1
+    up_parts = 2
     mix_parts = 2 if width % (8 * chips * 8) == 0 and width % 256 == 0 else 1
     parts = up_parts + mix_parts
     rows_in = width // (4 * chips * mix_parts)
     rows_out = -(-hidden // (4 * chips * 8)) * 8
     high = rows_out * 4 * chips
     dma = pltpu.SemaphoreType.DMA
-    steps = 2 * (chips - 1)
+    bits = chips.bit_length() - 1
     vmem = pl.BlockSpec(memory_space=pltpu.VMEM)
     hbm = pl.BlockSpec(memory_space=pl.ANY)
     shape = jax.ShapeDtypeStruct
     sizes = [(rows_out, width // up_parts)] * up_parts + [(rows_in, hidden)] * mix_parts
-    grad_inputs, small, *finals = pl.pallas_call(
+    grad_inputs, grad_kernel, grad_bias, *finals = pl.pallas_call(
         functools.partial(body, n, dp_size, rows_in, rows_out, up_parts, mix_parts),
-        out_shape=[shape((tokens, width), BF16), shape((16, width), F32)]
+        out_shape=[shape((tokens, width), BF16), shape((KW, width), F32), shape((1, hidden), F32)]
         + [shape((2, 2, chips) + size, BF16) for size in sizes],
         in_specs=[hbm] * 5 + [vmem],
-        out_specs=[vmem] * (2 + parts),
+        out_specs=[vmem] * (3 + parts),
         scratch_shapes=[pltpu.VMEM((4 * chips * r, c), F32) for r, c in sizes]
         + [pltpu.VMEM((2, chips) + size, BF16) for size in sizes] * 2
         + [pltpu.VMEM((2, chips - 1) + size, BF16) for size in sizes] * 2
@@ -569,8 +588,8 @@
             dma((parts, 2, n)), dma((parts, 2, n)),
             dma((2, n)), dma((2, n)),
             dma((parts,)), dma((parts,)),
-            dma((parts, 2, steps)), dma((parts, 2, steps)),
-            dma((parts, 2, chips)), dma((parts, 2, chips)),
+            dma((parts, 2, 2 * bits)), dma((parts, 2, 2 * bits)),
+            dma((parts, 2, bits + 1)), dma((parts, 2, bits + 1)),
             dma((2,)), dma((2,)),
             dma((n,)), dma((n,)),
             dma((dp_size,)), dma((dp_size,)),
@@ -592,8 +611,8 @@
         grad_inputs[None],
         jnp.concatenate(rows, axis=0).astype(F32),
         jnp.concatenate(columns, axis=1).astype(F32),
-        small[8, :hidden],
-        small[:KW],
+        grad_bias[0],
+        grad_kernel,
     )
 
 

time: 146 us -> 149 us (1.021)
  Pallas kernels: 132 us -> 138 us
  local copies, waits for them, and re-layouts: 3.58 us -> 1.41 us
    pallas_call x1, Pallas kernels: 132 us -> 138 us  [shards(): pl.pallas_call(functools.partial(body, n, dp_size, rows_in, rows_out, up_...]
    slice x2 -> x0, local copies, waits for them, and re-layouts: 2.79 us -> none  [the longest x1 1.4 us: shards(): small[:KW]]
where the time goes in v3:
time: 149 us
  Pallas kernels  138 us (93%)
  other arithmetic  9.53 us (6%)
    pallas_call x1, Pallas kernels, shards(): pl.pallas_call(functools.partial(body, n, dp_size, rows_in, rows_out, up_...  138 us
    convert_element_type x1, other arithmetic, shards(): jnp.concatenate(rows, axis=0).astype(F32)  8.91 us

profile of v3, /device:TPU:1, one launch (start us, length us, event | category | flops | bytes accessed | tf_op | source)
XLA Modules:
  0.0 149.2 jit_solution(6453232231372161688)
XLA Ops:
  0.6 137.6 %shard_map.101 = (bf16[192,1280]{1,0:T(8,128)(2,1)}, f32[7,1280]{1,0:T(8,128)}, f32[1,1280]{1,0:T(1,128)}, bf16[2,2,4,80,640]{4,3,2,1,0:T(8,128)(2,1)}, bf16[2,2...) custom-call(bf16[192,1280]{1,0:T(8,128)(2,1)} %bitcast.14, ...), custom_call_target="tpu_custom_call" | custom-call | tf_op jit(solution)/shard_map/pallas_call | solution.py:562
  138.2 0.0 copy-start.2
  138.3 0.0 copy-start
  138.3 0.0 copy-start.1
  138.3 8.9 %maximum_convert_fusion = (f32[1280,1280]{1,0:T(8,128)}, f32[1280,1280]{1,0:T(8,128)}) fusion(bf16[640,1280]{1,0:T(8,128)(2,1)} %bitcast.12, bf16[640,1280]{1,0:T(8,128)(2,1)} %bitcast.11, bf16[1280,640]{1,0:T(8,128)(2,1)} %bitcast.10, bf16[1280,640]{1,0:T(8,128)(2,1)} %bitcast.9), kind=kLoop, calls=%fused_computation | loop fusion | flops 13107200 | bytes 19660800 | tf_op jit(solution)/shard_map/convert_element_type | solution.py:612
  147.2 0.0 copy-done.2
  147.2 0.6 reduce
  147.8 0.0 copy-done
  147.8 0.8 copy.13
  148.6 0.0 copy-done.1
  148.6 0.6 copy.14
Async XLA Ops:
  138.2 8.9 %copy-start.2 = (f32[1,1280]{1,0:T(1,128)S(1)}, f32[1,1280]{1,0:T(1,128)}, u32[]{:S(2)}) copy-start(f32[1,1280]{1,0:T(1,128)} %get-tuple-element.17) | copy-start | bytes 15364
  138.3 9.6 %copy-start = (bf16[192,1280]{1,0:T(8,128)(2,1)S(1)}, bf16[192,1280]{1,0:T(8,128)(2,1)}, u32[]{:S(2)}) copy-start(bf16[192,1280]{1,0:T(8,128)(2,1)} %get-tuple-element.12) | copy-start | bytes 1474564
  138.3 10.3 %copy-start.1 = (f32[7,1280]{1,0:T(8,128)S(1)}, f32[7,1280]{1,0:T(8,128)}, u32[]{:S(2)}) copy-start(f32[7,1280]{1,0:T(8,128)} %get-tuple-element.30) | copy-start | bytes 107524

commit v4 on v3

--- a/solution.py
+++ b/solution.py
@@ -136,9 +136,8 @@
         dst = xpad.at[pl.ds(0 if d == 0 else EDGE + tokens, EDGE)]
         return send(src, dst, hs.at[d], hr.at[d], to)
 
-    for k in range(2):
-        for d in ways:
-            start(ahead[d] > 0, functools.partial(chain, k, d, 0))
+    for d in ways:
+        start(ahead[d] > 0, functools.partial(chain, 0, d, 0))
     for d in ways:
         start(ahead[d] > 0, functools.partial(x_edge, d))
     load_hidden(0).start()
@@ -199,13 +198,15 @@
             acc[at] += value
 
     def out_dot(c, b, first):
+        high = chunk_of(act.shape[2])
+
         def out_step(i, _):
-            at = pl.ds(pl.multiple_of(i * 128, 128), 128)
-            value = dot(act[b], up_all[c, b, :, at], ((0,), (0,)))
-            add_to(accs[c], (slice(None), at), value, first)
+            at = pl.ds(pl.multiple_of(i * high, high), high)
+            value = dot(act[b, :, at], up_all[c, b], ((0,), (0,)))
+            add_to(accs[c], (at, slice(None)), value, first)
             return 0
 
-        lax.fori_loop(0, up_wide // 128, out_step, 0)
+        lax.fori_loop(0, act.shape[2] // high, out_step, 0)
 
     def back_dot(b):
         def back_step(i, _):
@@ -381,7 +382,7 @@
                 active.remove(item)
 
     for k in range(parts):
-        follow = k + 2
+        follow = k + 1
         if k == 0:
             load_up(0).wait()
         use_own = functools.partial(use, k, me, True)

time: 149 us -> 142 us (0.953)
  Pallas kernels: 138 us -> 130 us
    pallas_call x1, Pallas kernels: 138 us -> 130 us  [shards(): pl.pallas_call(functools.partial(body, n, dp_size, rows_in, rows_out, up_...]
where the time goes in v4:
time: 142 us; the launch traced here: 141 us
  Pallas kernels  130 us (92%)
  other arithmetic  9.53 us (7%)
    pallas_call x1, Pallas kernels, shards(): pl.pallas_call(functools.partial(body, n, dp_size, rows_in, rows_out, up_...  130 us
    convert_element_type x1, other arithmetic, shards(): jnp.concatenate(rows, axis=0).astype(F32)  8.91 us

profile of v4, /device:TPU:1, one launch (start us, length us, event | category | flops | bytes accessed | tf_op | source)
XLA Modules:
  0.0 141.4 jit_solution(15027744512539155392)
XLA Ops:
  0.6 129.8 %shard_map.101 = (bf16[192,1280]{1,0:T(8,128)(2,1)}, f32[7,1280]{1,0:T(8,128)}, f32[1,1280]{1,0:T(1,128)}, bf16[2,2,4,80,640]{4,3,2,1,0:T(8,128)(2,1)}, bf16[2,2...) custom-call(bf16[192,1280]{1,0:T(8,128)(2,1)} %bitcast.14, ...), custom_call_target="tpu_custom_call" | custom-call | tf_op jit(solution)/shard_map/pallas_call | solution.py:563
  130.4 0.0 copy-start.2
  130.4 0.0 copy-start
  130.4 0.0 copy-start.1
  130.5 8.9 %maximum_convert_fusion = (f32[1280,1280]{1,0:T(8,128)}, f32[1280,1280]{1,0:T(8,128)}) fusion(bf16[640,1280]{1,0:T(8,128)(2,1)} %bitcast.12, bf16[640,1280]{1,0:T(8,128)(2,1)} %bitcast.11, bf16[1280,640]{1,0:T(8,128)(2,1)} %bitcast.10, bf16[1280,640]{1,0:T(8,128)(2,1)} %bitcast.9), kind=kLoop, calls=%fused_computation | loop fusion | flops 13107200 | bytes 19660800 | tf_op jit(solution)/shard_map/convert_element_type | solution.py:613
  139.4 0.0 copy-done.2
  139.4 0.6 reduce
  140.0 0.0 copy-done
  140.0 0.8 copy.13
  140.8 0.0 copy-done.1
  140.8 0.6 copy.14
Async XLA Ops:
  130.4 8.9 %copy-start.2 = (f32[1,1280]{1,0:T(1,128)S(1)}, f32[1,1280]{1,0:T(1,128)}, u32[]{:S(2)}) copy-start(f32[1,1280]{1,0:T(1,128)} %get-tuple-element.17) | copy-start | bytes 15364
  130.4 9.6 %copy-start = (bf16[192,1280]{1,0:T(8,128)(2,1)S(1)}, bf16[192,1280]{1,0:T(8,128)(2,1)}, u32[]{:S(2)}) copy-start(bf16[192,1280]{1,0:T(8,128)(2,1)} %get-tuple-element.12) | copy-start | bytes 1474564
  130.4 10.3 %copy-start.1 = (f32[7,1280]{1,0:T(8,128)S(1)}, f32[7,1280]{1,0:T(8,128)}, u32[]{:S(2)}) copy-start(f32[7,1280]{1,0:T(8,128)} %get-tuple-element.30) | copy-start | bytes 107524
